TPU v7x, 32 devices: a whole 2x2x4 slice. The times are simulated.
32 devices in a mesh: expert: 4 (over x, core), dp: 8 (over z, y).
Axes of the slice: x: 2, y: 2, z: 4, core: 2. Of those that a mesh axis runs over, the one named last changes fastest.
Arguments:
- cotangents: bfloat16 [4096, 2048], P(('expert', 'dp')), may hold values from -0.59765625 to 0.59765625
- routes: int32 [4096, 2], P(('expert', 'dp')), may hold values from 0 to 3, all different within a row; in each aligned block of 128 rows (0 to 127, 128 to 255, ...) at most 80 rows name the same one
- gate_probs: float32 [4096, 2], P(('expert', 'dp')), may hold values from 0.1 to 0.9
- hidden_now: bfloat16 [4, 8, 4, 80, 7168], P('expert', 'dp'), may hold values from -6 to 6
- hidden_prev: bfloat16 [4, 8, 4, 80, 7168], P('expert', 'dp'), may hold values from -6 to 6
- cotan_prev: bfloat16 [4, 8, 320, 2048], P('expert', 'dp'), may hold values from -0.29882812 to 0.29882812
- trigger: int32 [4, 8, 56], P('expert', 'dp'), may hold values from 0 to 1, as said below
- stale_sum: float32 [4, 7168, 2048], P('expert', None, 'dp'), may hold values from -12 to 12
Outputs:
- new_sum: float32 [4, 7168, 2048], P('expert', None, 'dp')
- margins: float32 [4, 8, 56], P('expert', 'dp')
Inputs may be any that keep to these rules, and one draw needn't show every extreme that they name: `routes`: in the rows of one device each expert is named at most 80 times. `trigger`: each worker's row of 56 entries holds between 1 and 16 ones, and some worker's row holds exactly 16.
All inputs are finite; a program needn't handle non-finite values.
Results may differ from a plain program's by a relative error of at most 0.0055.
Values may be sent and summed in bfloat16 or wider, within the bound.
A program may use at most 192 MiB of HBM per device.

v0:
```python
import jax
import jax.numpy as jnp
from jax import lax
from jax.sharding import PartitionSpec as P

DW = 2048
FFW = 7168
BLOCK = 128
TRIG = 16
BLOCKS = 56


trigger_weight = 0.1


def local(cotangents, routes, gate_probs, hidden_now, hidden_prev, cotan_prev, trigger, stale_sum):
    experts_here = lax.axis_size("expert")
    workers = lax.axis_size("dp")
    capacity = hidden_now.shape[3]
    columns = DW // workers
    flat_routes = routes.reshape(-1)
    onehot = (flat_routes[:, None] == jnp.arange(experts_here, dtype=jnp.int32)[None, :]).astype(
        jnp.int32
    )
    slot_ranks = jnp.sum((jnp.cumsum(onehot, axis=0) - 1) * onehot, axis=1)
    target = flat_routes * capacity + slot_ranks
    placing = jnp.where(
        jnp.arange(experts_here * capacity, dtype=jnp.int32)[:, None] == target[None, :],
        gate_probs.reshape(-1)[None, :],
        0.0,
    )
    repeated = jnp.repeat(cotangents.astype(jnp.float32), 2, axis=0)
    send_table = jnp.dot(placing, repeated, precision=lax.Precision.HIGHEST).astype(jnp.bfloat16)
    arrived = lax.all_to_all(
        send_table.reshape(experts_here, capacity, DW),
        "expert",
        split_axis=0,
        concat_axis=0,
        tiled=True,
    )
    stacked_left = jnp.concatenate(
        [hidden_now.reshape(-1, FFW), hidden_prev.reshape(-1, FFW)], axis=0
    )
    stacked_right = jnp.concatenate([arrived.reshape(-1, DW), -cotan_prev.reshape(-1, DW)], axis=0)
    difference = lax.dot_general(
        stacked_left, stacked_right, (((0,), (0,)), ((), ())), preferred_element_type=jnp.float32
    )
    blocks = difference.reshape(BLOCKS, BLOCK, DW)
    diff_norms = jnp.mean(blocks * blocks, axis=(1, 2))
    trigger_row = trigger.reshape(-1)
    running = jnp.cumsum(trigger_row)
    chosen = (trigger_row[None, :] == 1) & (
        running[None, :] == jnp.arange(1, TRIG + 1, dtype=jnp.int32)[:, None]
    )
    picked = jnp.sum(jnp.where(chosen, jnp.arange(BLOCKS, dtype=jnp.int32)[None, :], 0), axis=1)
    filled = jnp.any(chosen, axis=1)
    packed = jnp.where(filled[:, None, None], jnp.take(blocks, picked, axis=0), 0.0).astype(
        jnp.bfloat16
    )
    block_ids = jnp.broadcast_to(jnp.where(filled, picked, -1)[:, None, None], (TRIG, 1, workers))
    landed, landed_ids = (
        lax.all_to_all(packed, "dp", split_axis=2, concat_axis=0, tiled=True),
        lax.all_to_all(block_ids, "dp", split_axis=2, concat_axis=0, tiled=True),
    )
    placing_back = (
        jnp.arange(BLOCKS, dtype=jnp.int32)[:, None] == landed_ids.reshape(-1)[None, :]
    ).astype(jnp.bfloat16)
    summed = jnp.dot(
        placing_back, landed.reshape(landed.shape[0], -1), preferred_element_type=jnp.float32
    ).reshape(FFW, columns)
    new_block = stale_sum.reshape(FFW, columns) + summed
    squares = jnp.sum((new_block * new_block).reshape(BLOCKS, -1), axis=1)
    norm_totals = lax.psum(squares, "dp") / (BLOCK * DW)
    margins = diff_norms - trigger_weight * norm_totals
    return (new_block.reshape(1, FFW, columns), margins.reshape(1, 1, BLOCKS))


def solution(mesh):
    return jax.shard_map(
        local,
        mesh=mesh,
        in_specs=(
            P(("expert", "dp"), None),
            P(("expert", "dp"), None),
            P(("expert", "dp"), None),
            P("expert", "dp", None, None, None),
            P("expert", "dp", None, None, None),
            P("expert", "dp", None, None),
            P("expert", "dp", None),
            P("expert", None, "dp"),
        ),
        out_specs=(P("expert", None, "dp"), P("expert", "dp", None)),
        check_vma=False,
    )
```

profile of v0, /device:TPU:0, one launch (start us, length us, event | category | flops | bytes accessed | tf_op | source)
XLA Modules:
  0.0 370.1 jit_solution(9404306520295364343)
XLA Ops:
  0.7 0.9 copy.44
  1.5 0.1 eq.92
  1.7 0.1 reshape.144
  1.8 1.2 reduce-window.19
  3.5 2.1 broadcast_in_dim.78
  5.6 2.4 reshape.146
  8.0 0.8 copy.48
  8.8 0.1 broadcast_in_dim.75
  8.9 5.0 %convolution_convert_fusion = bf16[320,2048]{1,0:T(8,128)(2,1)} fusion(f32[256,2048]{1,0:T(8,128)} %reshape.146, f32[256]{0:T(256)S(1)} %broadcast_in_dim.75, s32[256]{0:T(256)S(1)} %multiply_add_fusion), kind=kOutput, calls=%fused_computation.8 | convolution fusion | flops 2014085120 | bytes 3409920 | tf_op jit(solution)/shard_map/dot_general | solution.py:33
  13.9 4.2 %all-to-all-start.1 = ((bf16[4,80,2048]{2,1,0:T(8,128)(2,1)}), bf16[4,80,2048]{2,1,0:T(8,128)(2,1)S(1)}, u32[]{:S(2)}, u32[]{:S(2)}) async-start(bf16[4,80,2048]{2,1,0:T(8,128)(2,1)} %bitcast.8), calls=%async_computation.1 | async-start | bytes 2621440 | tf_op jit(solution)/shard_map/all_to_all | solution.py:34
  18.3 0.1 reduce.2
  18.4 0.2 select_reduce_fusion
  18.6 0.2 fusion.13
  18.9 1.1 negate_bitcast_fusion
  20.0 15.4 %all-to-all-done.1 = bf16[4,80,2048]{2,1,0:T(8,128)(2,1)S(1)} async-done(((bf16[4,80,2048]{2,1,0:T(8,128)(2,1)}), bf16[4,80,2048]{2,1,0:T(8,128)(2,1)S(1)}, u32[]{:S(2)}, u32[]{:S(2)}) %all-to-all-start.1) | async-done | bytes 1310752 | tf_op jit(solution)/shard_map/all_to_all | solution.py:34
  35.4 0.6 broadcast_in_dim.72
  36.0 6.6 %all-to-all-start = ((s32[16,1,8]{0,1,2:T(1,128)}), s32[16,1,8]{0,1,2:T(1,128)S(1)}, u32[]{:S(2)}, u32[]{:S(2)}) async-start(s32[16,1,8]{0,1,2:T(1,128)} %broadcast_in_dim.72), calls=%async_computation | async-start | bytes 8192 | tf_op jit(solution)/shard_map/all_to_all | solution.py:63
  42.6 29.1 %multiply_reduce_fusion = (f32[7168]{0:T(1024)S(1)}, bf16[7168,2048]{1,0:T(8,128)(2,1)}) fusion(bf16[320,2048]{1,0:T(8,128)(2,1)} %negate_bitcast_fusion, bf16[320,2048]{1,0:T(8,128)(2,1)S(1)} %bitcast.51, bf16[320,7168]{1,0:T(8,128)(2,1)} %bitcast.55, bf16[320,7168]{1,0:T(8,128)(2,1)} %bitcast.56), kind=kOutput, calls=%fused_computation.1 | convolution fusion | flops 18858106880 | bytes 41185280 | tf_op jit(solution)/shard_map/dot_general | solution.py:45
  71.6 14.2 %gather_fusion = bf16[16,128,2048]{2,1,0:T(8,128)(2,1)} fusion(bf16[56,128,2048]{2,1,0:T(8,128)(2,1)} %bitcast.50, s32[1024]{0:T(1024)S(1)} %pad_clamp_fusion), kind=kCustom, calls=%fused_computation | custom fusion | bytes 16777280 | tf_op jit(solution)/shard_map/jit(_take)/gather | solution.py:57
  85.9 10.4 %select_convert_fusion = bf16[16,128,2048]{2,1,0:T(8,128)(2,1)} fusion(bf16[16,128,2048]{2,1,0:T(8,128)(2,1)} %gather_fusion, pred[16]{0:T(512)(128)(4,1)S(1)} %compare_and_fusion.1, pred[16]{0:T(512)(128)(4,1)S(1)} %fusion.13), kind=kLoop, calls=%fused_computation.2 | loop fusion | flops 8388608 | bytes 16777248 | tf_op jit(solution)/shard_map/convert_element_type | solution.py:57
  96.3 12.4 %copy.49 = bf16[16,128,2048]{1,0,2:T(8,128)(2,1)} copy(bf16[16,128,2048]{2,1,0:T(8,128)(2,1)} %select_convert_fusion) | data formatting | bytes 16777216 | tf_op jit(solution)/shard_map/convert_element_type | solution.py:57
  108.7 5.8 %all-to-all-start.2 = ((bf16[16,128,2048]{1,0,2:T(8,128)(2,1)}), bf16[16,128,2048]{1,0,2:T(8,128)(2,1)}, u32[]{:S(2)}, u32[]{:S(2)}) async-start(bf16[16,128,2048]{1,0,2:T(8,128)(2,1)} %copy.49), calls=%async_computation.2 | async-start | bytes 16777216 | tf_op jit(solution)/shard_map/all_to_all | solution.py:62
  114.5 9.0 %reshape.152 = f32[56,32768]{1,0:T(8,128)} reshape(f32[1,7168,256]{2,1,0:T(8,128)} %param.15) | data formatting | bytes 14680064 | tf_op jit(solution)/shard_map/reshape | solution.py:71
  123.6 0.1 bitcast_reduce_fusion
  123.7 173.2 %all-to-all-done.2 = bf16[16,128,2048]{1,0,2:T(8,128)(2,1)} async-done(((bf16[16,128,2048]{1,0,2:T(8,128)(2,1)}), bf16[16,128,2048]{1,0,2:T(8,128)(2,1)}, u32[]{:S(2)}, u32[]{:S(2)}) %all-to-all-start.2) | async-done | bytes 8388640 | tf_op jit(solution)/shard_map/all_to_all | solution.py:62
  296.9 12.7 %copy.51 = bf16[8,16,128,256]{3,2,1,0:T(8,128)(2,1)} copy(bf16[8,16,128,256]{2,1,3,0:T(8,128)(2,1)} %bitcast.16) | data formatting | bytes 16777216 | tf_op jit(solution)/shard_map/all_to_all | solution.py:62
  309.6 12.3 %copy.54 = bf16[16,8,128,256]{3,1,2,0:T(8,128)(2,1)} copy(bf16[16,8,128,256]{3,2,1,0:T(8,128)(2,1)} %bitcast.49) | data formatting | bytes 16777216
  321.9 10.1 %multiply_reduce_fusion.1 = (f32[56]{0:T(128)S(1)}, f32[56,32768]{1,0:T(8,128)}) fusion(f32[56,32768]{1,0:T(8,128)} %reshape.152, bf16[128,32768]{1,0:T(8,128)(2,1)} %bitcast.48, s32[128]{0:T(128)S(1)} %eq.85), kind=kOutput, calls=%fused_computation.7 | convolution fusion | flops 475274176 | bytes 23069408 | tf_op jit(solution)/shard_map/dot_general | solution.py:68
  332.0 19.5 %psum.7 = f32[56]{0:T(128)S(1)} all-reduce(f32[56]{0:T(128)S(1)} %get-tuple-element.2), channel_id=1, replica_groups=mesh['expert'=4,'dp'=8] {'dp'}, use_global_device_ids=true, to_apply=%region_9.10 | all-reduce | flops 56 | bytes 448 | tf_op jit(solution)/shard_map/psum | solution.py:73
  351.5 8.9 %reshape.151 = f32[1,7168,256]{2,1,0:T(8,128)} reshape(f32[56,32768]{1,0:T(8,128)} %get-tuple-element.3) | data formatting | bytes 14680064 | tf_op jit(solution)/shard_map/reshape | solution.py:70
  360.4 9.2 %add.45 = f32[1,7168,256]{2,1,0:T(8,128)} add(f32[1,7168,256]{2,1,0:T(8,128)} %param.15, f32[1,7168,256]{2,1,0:T(8,128)} %reshape.151) | non-fusion elementwise | flops 1835008 | bytes 22020096 | tf_op jit(solution)/shard_map/add | solution.py:71
  369.6 0.5 subtract_bitcast_fusion
  (23 shorter events, 0.7 us)
Async XLA Ops:
  0.6 17.5 %copy-start.1 = (s32[1,1,56]{2,1,0:T(1,128)S(1)}, s32[1,1,56]{2,1,0:T(1,128)}, u32[]{:S(2)}) copy-start(s32[1,1,56]{2,1,0:T(1,128)} %param.14) | copy-start | bytes 676
  0.6 18.2 %copy-start = (bf16[1,1,320,2048]{3,2,1,0:T(8,128)(2,1)S(1)}, bf16[1,1,320,2048]{3,2,1,0:T(8,128)(2,1)}, u32[]{:S(2)}) copy-start(bf16[1,1,320,2048]{3,2,1,0:T(8,128)(2,1)} %param.13) | copy-start | bytes 3932164
  13.9 21.5 %all-to-all-start.1 = ((bf16[4,80,2048]{2,1,0:T(8,128)(2,1)}), bf16[4,80,2048]{2,1,0:T(8,128)(2,1)S(1)}, u32[]{:S(2)}, u32[]{:S(2)}) async-start(bf16[4,80,2048]{2,1,0:T(8,128)(2,1)} %bitcast.8), calls=%async_computation.1 | async-start | bytes 2621440 | tf_op jit(solution)/shard_map/all_to_all | solution.py:34
  36.0 72.8 %all-to-all-start = ((s32[16,1,8]{0,1,2:T(1,128)}), s32[16,1,8]{0,1,2:T(1,128)S(1)}, u32[]{:S(2)}, u32[]{:S(2)}) async-start(s32[16,1,8]{0,1,2:T(1,128)} %broadcast_in_dim.72), calls=%async_computation | async-start | bytes 8192 | tf_op jit(solution)/shard_map/all_to_all | solution.py:63
  108.7 188.1 %all-to-all-start.2 = ((bf16[16,128,2048]{1,0,2:T(8,128)(2,1)}), bf16[16,128,2048]{1,0,2:T(8,128)(2,1)}, u32[]{:S(2)}, u32[]{:S(2)}) async-start(bf16[16,128,2048]{1,0,2:T(8,128)(2,1)} %copy.49), calls=%async_computation.2 | async-start | bytes 16777216 | tf_op jit(solution)/shard_map/all_to_all | solution.py:62
where the time goes:
time: 372 us; the launch traced here: 370 us
  waiting for transfers between devices  189 us (51%)
  local copies, waits for them, and re-layouts  77.3 us (21%)
  matrix products  44.1 us (12%)
  other arithmetic  23.3 us (6%)
  blocking collectives  19.5 us (5%)
  starting transfers between devices  16.6 us (4%)
    all_to_all x1, waiting for transfers between devices, local(): lax.all_to_all(packed, 'dp', split_axis=2, concat_axis=0, tiled=True)  173 us
    dot_general x1, matrix products, local(): lax.dot_general(stacked_left, stacked_right, (((0,), (0,)), ((), ())), pr...  29.1 us
    psum x1, blocking collectives, local(): norm_totals = lax.psum(squares, 'dp') / (BLOCK * DW)  19.5 us
    all_to_all x1, waiting for transfers between devices, local(): lax.all_to_all(send_table.reshape(experts_here, capacity, DW), 'expert',...  15.4 us
    gather x1, local copies, waits for them, and re-layouts, local(): jnp.take(blocks, picked, axis=0)  14.2 us
    unnamed x7, local copies, waits for them, and re-layouts  14 us
    all_to_all x1, local copies, waits for them, and re-layouts, local(): lax.all_to_all(packed, 'dp', split_axis=2, concat_axis=0, tiled=True)  12.7 us
    convert_element_type x1, local copies, waits for them, and re-layouts, local(): jnp.where(filled[:, None, None], jnp.take(blocks, picked, axis=0), 0.0)  12.4 us
  transfers between devices with their start and end apart: 3, of which 2 were waited for; matrix products, arithmetic and copies ran while one was open for 21% of the time, Pallas kernels for 0%

commit v1 on v0

v1 whole, which is shorter than its diff:
```python
import functools

import jax
import jax.numpy as jnp
from jax import lax
from jax.experimental import pallas as pl
from jax.experimental.pallas import tpu as pltpu
from jax.sharding import PartitionSpec as P

BLOCK = 128
TRIG = 16
LANES = 128
trigger_weight = 0.1
MESH = pl.DeviceIdType.MESH
TN = (((0,), (0,)), ((), ()))


def params(**kw):
    return pltpu.CompilerParams(vmem_limit_bytes=60 * 1024 * 1024, **kw)


def greet(axis, n, me):
    barrier = pltpu.get_barrier_semaphore()
    for step in range(1, n):
        pl.semaphore_signal(
            barrier, inc=1, device_id={axis: lax.rem(me + step, n)}, device_id_type=MESH
        )
    pl.semaphore_wait(barrier, n - 1)


def table_kernel(n, capacity, routes_ref, gates_ref, cotan_ref, out_ref):
    tokens = cotan_ref.shape[0]
    experts = lax.broadcasted_iota(jnp.int32, (n, tokens), 0)
    first = routes_ref[0:1, :] == experts
    second = routes_ref[1:2, :] == experts
    named = jnp.where(first | second, 1.0, 0.0)
    gates = jnp.where(first, gates_ref[0:1, :], 0.0) + jnp.where(second, gates_ref[1:2, :], 0.0)
    earlier = jnp.where(
        lax.broadcasted_iota(jnp.int32, (tokens, tokens), 0)
        < lax.broadcasted_iota(jnp.int32, (tokens, tokens), 1),
        1.0,
        0.0,
    )
    ranks = jnp.dot(
        named.astype(jnp.bfloat16), earlier.astype(jnp.bfloat16), preferred_element_type=jnp.float32
    )
    ranks = jnp.where(named > 0.5, ranks, -1.0)
    slot = lax.broadcasted_iota(jnp.int32, (capacity, tokens), 0).astype(jnp.float32)
    for e in range(n):
        place = jnp.where(slot == ranks[e : e + 1, :], 1.0, 0.0)
        weight = jnp.sum(place * gates[e : e + 1, :], axis=1, keepdims=True)
        rows = jnp.dot(
            place.astype(jnp.bfloat16), cotan_ref[...], preferred_element_type=jnp.float32
        )
        out_ref[e] = (rows * weight).astype(jnp.bfloat16)


def exchange_kernel(n, table_ref, out_ref, own_sem, send_sem, recv_sem):
    me = lax.axis_index("expert")
    greet("expert", n, me)
    copies = []
    for step in range(1, n):
        peer = lax.rem(me + step, n)
        copy = pltpu.make_async_remote_copy(
            src_ref=table_ref.at[peer],
            dst_ref=out_ref.at[me],
            send_sem=send_sem.at[step],
            recv_sem=recv_sem.at[step],
            device_id={"expert": peer},
            device_id_type=MESH,
        )
        copy.start()
        copies.append(copy)
    own = pltpu.make_async_copy(table_ref.at[me], out_ref.at[me], own_sem)
    own.start()
    own.wait()
    for copy in copies:
        copy.wait()


def dispatch(routes, gates, cotangents, n, capacity):
    width = cotangents.shape[1]
    shape = jax.ShapeDtypeStruct((n, capacity, width), jnp.bfloat16)
    table = pl.pallas_call(
        functools.partial(table_kernel, n, capacity),
        out_shape=shape,
        compiler_params=params(),
        name="table",
    )(routes, gates, cotangents)
    return pl.pallas_call(
        functools.partial(exchange_kernel, n),
        out_shape=shape,
        in_specs=[pl.BlockSpec(memory_space=pltpu.VMEM)],
        out_specs=pl.BlockSpec(memory_space=pltpu.VMEM),
        scratch_shapes=[
            pltpu.SemaphoreType.DMA,
            pltpu.SemaphoreType.DMA((n,)),
            pltpu.SemaphoreType.DMA((n,)),
        ],
        compiler_params=params(collective_id=0, has_side_effects=True),
        name="exchange",
    )(table)


def picked_kernel(parts, picked_ref, now_ref, prev_ref, arrived_ref, cotan_ref, out_ref):
    columns = out_ref.shape[-1]
    per = 4 if parts % 4 == 0 else 1
    wide = columns * parts // per
    keep = jnp.where(picked_ref[1, pl.program_id(0)] > 0, 1.0, 0.0)
    for q in range(per):
        cut = slice(q * wide, (q + 1) * wide)
        total = lax.dot_general(
            now_ref[...], arrived_ref[:, cut], TN, preferred_element_type=jnp.float32
        ) - lax.dot_general(
            prev_ref[...], cotan_ref[:, cut], TN, preferred_element_type=jnp.float32
        )
        total = (total * keep).astype(jnp.bfloat16)
        for p in range(parts // per):
            out_ref[q * (parts // per) + p, 0] = total[:, p * columns : (p + 1) * columns]


def picked_blocks(picked, now, prev, arrived, cotan, parts):
    rows, width = arrived.shape
    columns = width // parts
    return pl.pallas_call(
        functools.partial(picked_kernel, parts),
        out_shape=jax.ShapeDtypeStruct((parts, TRIG, BLOCK, columns), jnp.bfloat16),
        grid_spec=pltpu.PrefetchScalarGridSpec(
            num_scalar_prefetch=1,
            grid=(TRIG,),
            in_specs=[
                pl.BlockSpec((rows, BLOCK), lambda k, ids: (0, ids[0, k])),
                pl.BlockSpec((rows, BLOCK), lambda k, ids: (0, ids[0, k])),
                pl.BlockSpec((rows, width), lambda k, ids: (0, 0)),
                pl.BlockSpec((rows, width), lambda k, ids: (0, 0)),
            ],
            out_specs=pl.BlockSpec((parts, 1, BLOCK, columns), lambda k, ids: (0, k, 0, 0)),
        ),
        compiler_params=params(dimension_semantics=("arbitrary",)),
        cost_estimate=pl.CostEstimate(
            flops=4 * TRIG * BLOCK * rows * width, bytes_accessed=4 * TRIG * BLOCK * width, transcendentals=0
        ),
        name="picked",
    )(picked, now, prev, arrived, cotan)


def norms_kernel(group, now_ref, prev_ref, arrived_ref, cotan_ref, out_ref):
    width = arrived_ref.shape[1]
    step = 512 if width % 512 == 0 else width
    sums = [jnp.zeros((1, LANES), jnp.float32) for _ in range(group)]
    for q in range(width // step):
        cut = slice(q * step, (q + 1) * step)
        total = lax.dot_general(
            now_ref[...], arrived_ref[:, cut], TN, preferred_element_type=jnp.float32
        ) - lax.dot_general(
            prev_ref[...], cotan_ref[:, cut], TN, preferred_element_type=jnp.float32
        )
        square = total * total
        for g in range(group):
            part = jnp.sum(square[g * BLOCK : (g + 1) * BLOCK], axis=0, keepdims=True)
            for i in range(step // LANES):
                sums[g] = sums[g] + part[:, i * LANES : (i + 1) * LANES]
    for g in range(group):
        out_ref[g] = sums[g]


def block_norms(now, prev, arrived, cotan):
    rows, width = arrived.shape
    blocks = now.shape[1] // BLOCK
    group = 4 if blocks % 4 == 0 else 1
    return pl.pallas_call(
        functools.partial(norms_kernel, group),
        out_shape=jax.ShapeDtypeStruct((blocks, 1, LANES), jnp.float32),
        grid=(blocks // group,),
        in_specs=[
            pl.BlockSpec((rows, group * BLOCK), lambda b: (0, b)),
            pl.BlockSpec((rows, group * BLOCK), lambda b: (0, b)),
            pl.BlockSpec((rows, width), lambda b: (0, 0)),
            pl.BlockSpec((rows, width), lambda b: (0, 0)),
        ],
        out_specs=pl.BlockSpec((group, 1, LANES), lambda b: (b, 0, 0)),
        compiler_params=params(dimension_semantics=("arbitrary",)),
        cost_estimate=pl.CostEstimate(
            flops=4 * now.shape[1] * rows * width, bytes_accessed=4 * now.size, transcendentals=0
        ),
        name="norms",
    )(now, prev, arrived, cotan)


def add_kernel(workers, table_ref, stale_ref, landed_ref, out_ref, square_ref):
    b = pl.program_id(0)
    out_ref[...] = stale_ref[...]
    for w in range(workers):
        index = table_ref[w, b]

        @pl.when(index >= 0)
        def _():
            out_ref[0] += landed_ref[w, index].astype(jnp.float32)

    new = out_ref[0]
    part = jnp.sum(new * new, axis=0, keepdims=True)
    total = part[:, 0:LANES]
    for i in range(1, new.shape[1] // LANES):
        total = total + part[:, i * LANES : (i + 1) * LANES]
    square_ref[0] = total


def add_landed(table, stale, landed):
    workers, slots, _, columns = landed.shape
    blocks = stale.shape[0]
    return pl.pallas_call(
        functools.partial(add_kernel, workers),
        out_shape=(
            jax.ShapeDtypeStruct(stale.shape, jnp.float32),
            jax.ShapeDtypeStruct((blocks, 1, LANES), jnp.float32),
        ),
        grid_spec=pltpu.PrefetchScalarGridSpec(
            num_scalar_prefetch=1,
            grid=(blocks,),
            in_specs=[
                pl.BlockSpec((1, BLOCK, columns), lambda b, ids: (b, 0, 0)),
                pl.BlockSpec((workers, slots, BLOCK, columns), lambda b, ids: (0, 0, 0, 0)),
            ],
            out_specs=(
                pl.BlockSpec((1, BLOCK, columns), lambda b, ids: (b, 0, 0)),
                pl.BlockSpec((1, 1, LANES), lambda b, ids: (b, 0, 0)),
            ),
        ),
        compiler_params=params(dimension_semantics=("arbitrary",)),
        cost_estimate=pl.CostEstimate(flops=4 * stale.size, bytes_accessed=10 * stale.size, transcendentals=0),
        name="addlanded",
    )(table, stale, landed)


def total_kernel(n, part_ref, out_ref, landed, send_sem, recv_sem):
    me = lax.axis_index("dp")
    greet("dp", n, me)
    copies = []
    for step in range(1, n):
        copy = pltpu.make_async_remote_copy(
            src_ref=part_ref,
            dst_ref=landed.at[step],
            send_sem=send_sem.at[step],
            recv_sem=recv_sem.at[step],
            device_id={"dp": lax.rem(me + step, n)},
            device_id_type=MESH,
        )
        copy.start()
        copies.append(copy)
    for copy in copies:
        copy.wait()
    total = part_ref[...]
    for step in range(1, n):
        total = total + landed[step]
    out_ref[...] = total


def shared_total(part, n):
    return pl.pallas_call(
        functools.partial(total_kernel, n),
        out_shape=jax.ShapeDtypeStruct(part.shape, jnp.float32),
        in_specs=[pl.BlockSpec(memory_space=pltpu.VMEM)],
        out_specs=pl.BlockSpec(memory_space=pltpu.VMEM),
        scratch_shapes=[
            pltpu.VMEM((n,) + part.shape, jnp.float32),
            pltpu.SemaphoreType.DMA((n,)),
            pltpu.SemaphoreType.DMA((n,)),
        ],
        compiler_params=params(collective_id=1, has_side_effects=True),
        name="total",
    )(part)


def local(cotangents, routes, gate_probs, hidden_now, hidden_prev, cotan_prev, trigger, stale_sum):
    experts = lax.axis_size("expert")
    workers = lax.axis_size("dp")
    capacity, ffw = hidden_now.shape[3:]
    width = cotangents.shape[1]
    columns = width // workers
    blocks = ffw // BLOCK
    now = hidden_now.reshape(-1, ffw)
    prev = hidden_prev.reshape(-1, ffw)
    cotan = cotan_prev.reshape(-1, width)

    row = trigger.reshape(-1)
    running = jnp.cumsum(row)
    order = jnp.arange(1, TRIG + 1, dtype=jnp.int32)[:, None]
    chosen = (row[None, :] == 1) & (running[None, :] == order)
    ids = jnp.sum(jnp.where(chosen, jnp.arange(blocks, dtype=jnp.int32)[None, :], 0), axis=1)
    filled = jnp.sum(chosen.astype(jnp.int32), axis=1)
    rows = lax.all_gather(row, "dp")
    table = jnp.where(rows == 1, jnp.cumsum(rows, axis=1) - 1, -1)

    arrived = dispatch(routes.T, gate_probs.T, cotangents, experts, capacity).reshape(-1, width)
    packed = picked_blocks(jnp.stack([ids, filled]), now, prev, arrived, cotan, workers)
    landed = lax.all_to_all(packed, "dp", split_axis=0, concat_axis=0, tiled=True)
    norms = block_norms(now, prev, arrived, cotan)
    new, squares = add_landed(table, stale_sum.reshape(blocks, BLOCK, columns), landed)
    totals = shared_total(squares.reshape(blocks, LANES), workers)
    margins = jnp.sum(norms.reshape(blocks, LANES) - trigger_weight * totals, axis=1) / (BLOCK * width)
    return new.reshape(1, ffw, columns), margins.reshape(1, 1, blocks)


def solution(mesh):
    return jax.shard_map(
        local,
        mesh=mesh,
        in_specs=(
            P(("expert", "dp"), None),
            P(("expert", "dp"), None),
            P(("expert", "dp"), None),
            P("expert", "dp", None, None, None),
            P("expert", "dp", None, None, None),
            P("expert", "dp", None, None),
            P("expert", "dp", None),
            P("expert", None, "dp"),
        ),
        out_specs=(P("expert", None, "dp"), P("expert", "dp", None)),
        check_vma=False,
    )
```

time: 372 us -> 325 us (0.87)
  waiting for transfers between devices: 189 us -> 0.01 us
  Pallas kernels: 0 us -> 158 us
  blocking collectives: 19.5 us -> 152 us
  local copies, waits for them, and re-layouts: 77.3 us -> 0.75 us
  matrix products: 44.1 us -> 0 us
  other arithmetic: 23.3 us -> 3.81 us
  starting transfers between devices: 16.6 us -> 7.48 us
    all_to_all x3 -> x1, waiting for transfers between devices: 189 us -> 0.01 us  [local(): lax.all_to_all(packed, 'dp', split_axis=0, concat_axis=0, tiled=True)]
    pallas_call x0 -> x6, Pallas kernels: none -> 158 us  [the longest x1 48.5 us: shared_total(): pl.pallas_call(functools.partial(total_kernel, n), out_shape=jax.ShapeDty...]
    all_gather x0 -> x1, blocking collectives: none -> 152 us  [local(): rows = lax.all_gather(row, 'dp')]
    dot_general x3 -> x0, matrix products: 44.1 us -> none  [the longest x1 29.1 us: local(): lax.dot_general(stacked_left, stacked_right, (((0,), (0,)), ((), ())), pr...]
    reshape x4 -> x0, local copies, waits for them, and re-layouts: 20.5 us -> none  [the longest x1 9.01 us: local(): new_block = stale_sum.reshape(FFW, columns) + summed]
    psum x1 -> x0, blocking collectives: 19.5 us -> none  [local(): norm_totals = lax.psum(squares, 'dp') / (BLOCK * DW)]
    gather x1 -> x0, local copies, waits for them, and re-layouts: 14.2 us -> none  [local(): jnp.take(blocks, picked, axis=0)]
    unnamed x7 -> x4, local copies, waits for them, and re-layouts: 14 us -> 0.01 us
  transfers between devices with their start and end apart: 3 -> 1, of which waited for: 2 -> 0; matrix products, arithmetic and copies ran while one was open for 21% -> 0% of each run, Pallas kernels for 0% -> 11%
where the time goes in v1:
time: 325 us; the launch traced here: 323 us
  Pallas kernels  158 us (49%)
  blocking collectives  152 us (47%)
  starting transfers between devices  7.48 us (2%)
  other arithmetic  3.81 us (1%)
    all_gather x1, blocking collectives, local(): rows = lax.all_gather(row, 'dp')  152 us
    pallas_call x1, Pallas kernels, shared_total(): pl.pallas_call(functools.partial(total_kernel, n), out_shape=jax.ShapeDty...  48.5 us
    pallas_call x1, Pallas kernels, block_norms(): pl.pallas_call(functools.partial(norms_kernel, group), out_shape=jax.Shap...  36.3 us
    pallas_call x1, Pallas kernels, add_landed(): pl.pallas_call(functools.partial(add_kernel, workers), out_shape=(jax.Sha...  34.7 us
    pallas_call x1, Pallas kernels, dispatch(): pl.pallas_call(functools.partial(exchange_kernel, n), out_shape=shape, in...  20 us
    pallas_call x1, Pallas kernels, picked_blocks(): pl.pallas_call(functools.partial(picked_kernel, parts), out_shape=jax.Sha...  16.2 us
    all_to_all x1, starting transfers between devices, local(): lax.all_to_all(packed, 'dp', split_axis=0, concat_axis=0, tiled=True)  7.48 us
  transfers between devices with their start and end apart: 1, of which 0 were waited for; matrix products, arithmetic and copies ran while one was open for 0% of the time, Pallas kernels for 11%

profile of v1, /device:TPU:0, one launch (start us, length us, event | category | flops | bytes accessed | tf_op | source)
XLA Modules:
  0.0 322.8 jit_solution(10660872297929775275)
XLA Ops:
  0.6 0.7 compare_bitcast_fusion
  1.3 0.7 copy.15
  2.0 0.1 reduce-window.8
  2.1 0.1 reduce
  2.2 2.8 table.1.table_ref
  5.0 20.0 %exchange.1 = bf16[4,80,2048]{2,1,0:T(8,128)(2,1)} custom-call(bf16[4,80,2048]{2,1,0:T(8,128)(2,1)} %table.1.table_ref), custom_call_target="tpu_custom_call" | custom-call | tf_op jit(solution)/shard_map/exchange/pallas_call | solution.py:90
  25.0 0.2 select_reduce_fusion
  25.2 0.6 pad_add_fusion.picked_ref
  25.8 16.2 %picked.1 = bf16[8,16,128,256]{3,2,1,0:T(8,128)(2,1)} custom-call(s32[2,16]{1,0:T(2,128)} %pad_add_fusion.picked_ref, bf16[320,7168]{1,0:T(8,128)(2,1)} %bitcast.21, bf16[320,7168]{1,0:T(8,128)(2,1)} %bitcast.23, bf16[320,2048]{1,0:T(8,128)(2,1)} %bitcast.19, bf16[320,2048]{1,0:T(8,128)(2,1)} %bitcast.25), custom_call_target="tpu_custom_call" | custom-call | flops 5368709120 | bytes 16777216 | tf_op jit(solution)/shard_map/picked/pallas_call | solution.py:125
  42.0 0.0 copy-start.1
  42.0 7.5 %all-to-all-start = ((bf16[8,16,128,256]{3,2,1,0:T(8,128)(2,1)}), bf16[8,16,128,256]{3,2,1,0:T(8,128)(2,1)}, u32[]{:S(2)}, u32[]{:S(2)}) async-start(bf16[8,16,128,256]{3,2,1,0:T(8,128)(2,1)} %picked.1), calls=%async_computation | async-start | bytes 16777216 | tf_op jit(solution)/shard_map/all_to_all | solution.py:296
  49.5 0.0 copy-done.1
  49.5 151.6 %all-gather = s32[8,1,56]{2,1,0:T(1,128)S(1)} all-gather(s32[1,1,56]{2,1,0:T(1,128)S(1)} %copy-done.1), channel_id=2, replica_groups=mesh['expert'=4,'dp'=8] {'dp'}, dimensions={0}, use_global_device_ids=true | all-gather | bytes 2016 | tf_op jit(solution)/shard_map/all_gather | solution.py:291
  201.1 0.2 reduce_window_sum.18
  201.3 0.6 add_select_fusion.table_ref
  201.9 36.3 %norms.1 = f32[56,1,128]{2,1,0:T(1,128)} custom-call(bf16[320,7168]{1,0:T(8,128)(2,1)} %bitcast.22, bf16[320,7168]{1,0:T(8,128)(2,1)} %bitcast.24, bf16[320,2048]{1,0:T(8,128)(2,1)} %bitcast.20, bf16[320,2048]{1,0:T(8,128)(2,1)} %bitcast.26), custom_call_target="tpu_custom_call" | custom-call | flops 18790481920 | bytes 9175040 | tf_op jit(solution)/shard_map/norms/pallas_call | solution.py:171
  238.2 0.0 all-to-all-done.landed_ref
  238.2 0.0 copy-start
  238.2 34.7 %addlanded.1 = (f32[56,128,256]{2,1,0:T(8,128)}, f32[56,1,128]{2,1,0:T(1,128)}) custom-call(s32[8,56]{1,0:T(8,128)} %add_select_fusion.table_ref, f32[56,128,256]{2,1,0:T(8,128)} %bitcast.18, bf16[8,16,128,256]{3,2,1,0:T(8,128)(2,1)} %all-to-all-done.landed_ref), custom_call_target="tpu_custom_call" | custom-call | flops 7340032 | bytes 18350080 | tf_op jit(solution)/shard_map/addlanded/pallas_call | solution.py:211
  272.9 48.5 %total.1 = f32[56,128]{1,0:T(8,128)} custom-call(f32[56,128]{1,0:T(8,128)} %bitcast.30), custom_call_target="tpu_custom_call" | custom-call | tf_op jit(solution)/shard_map/total/pallas_call | solution.py:259
  321.4 0.0 copy-done
  321.4 0.9 subtract_reduce_fusion
  322.3 0.5 multiply_bitcast_fusion
  (1 shorter events, 0.0 us)
Async XLA Ops:
  42.0 7.5 %copy-start.1 = (s32[1,1,56]{2,1,0:T(1,128)S(1)}, s32[1,1,56]{2,1,0:T(1,128)}, u32[]{:S(2)}) copy-start(s32[1,1,56]{2,1,0:T(1,128)} %param.14) | copy-start | bytes 676
  42.0 196.2 %all-to-all-start = ((bf16[8,16,128,256]{3,2,1,0:T(8,128)(2,1)}), bf16[8,16,128,256]{3,2,1,0:T(8,128)(2,1)}, u32[]{:S(2)}, u32[]{:S(2)}) async-start(bf16[8,16,128,256]{3,2,1,0:T(8,128)(2,1)} %picked.1), calls=%async_computation | async-start | bytes 16777216 | tf_op jit(solution)/shard_map/all_to_all | solution.py:296
  238.2 83.2 %copy-start = (f32[56,1,128]{2,1,0:T(1,128)S(1)}, f32[56,1,128]{2,1,0:T(1,128)}, u32[]{:S(2)}) copy-start(f32[56,1,128]{2,1,0:T(1,128)} %norms.1) | copy-start | bytes 86020

commit v2 on v1

--- a/solution.py
+++ b/solution.py
@@ -187,43 +187,45 @@
     )(now, prev, arrived, cotan)
 
 
-def add_kernel(workers, table_ref, stale_ref, landed_ref, out_ref, square_ref):
-    b = pl.program_id(0)
+def add_kernel(workers, group, table_ref, stale_ref, landed_ref, out_ref, square_ref):
     out_ref[...] = stale_ref[...]
-    for w in range(workers):
-        index = table_ref[w, b]
-
-        @pl.when(index >= 0)
-        def _():
-            out_ref[0] += landed_ref[w, index].astype(jnp.float32)
-
-    new = out_ref[0]
-    part = jnp.sum(new * new, axis=0, keepdims=True)
-    total = part[:, 0:LANES]
-    for i in range(1, new.shape[1] // LANES):
-        total = total + part[:, i * LANES : (i + 1) * LANES]
-    square_ref[0] = total
+    for g in range(group):
+        b = pl.program_id(0) * group + g
+        for w in range(workers):
+            index = table_ref[w, b]
+
+            @pl.when(index >= 0)
+            def _():
+                out_ref[g] += landed_ref[w, index].astype(jnp.float32)
+
+        new = out_ref[g]
+        part = jnp.sum(new * new, axis=0, keepdims=True)
+        total = part[:, 0:LANES]
+        for i in range(1, new.shape[1] // LANES):
+            total = total + part[:, i * LANES : (i + 1) * LANES]
+        square_ref[g] = total
 
 
 def add_landed(table, stale, landed):
     workers, slots, _, columns = landed.shape
     blocks = stale.shape[0]
-    return pl.pallas_call(
-        functools.partial(add_kernel, workers),
+    group = 4 if blocks % 4 == 0 else 1
+    return pl.pallas_call(
+        functools.partial(add_kernel, workers, group),
         out_shape=(
             jax.ShapeDtypeStruct(stale.shape, jnp.float32),
             jax.ShapeDtypeStruct((blocks, 1, LANES), jnp.float32),
         ),
         grid_spec=pltpu.PrefetchScalarGridSpec(
             num_scalar_prefetch=1,
-            grid=(blocks,),
+            grid=(blocks // group,),
             in_specs=[
-                pl.BlockSpec((1, BLOCK, columns), lambda b, ids: (b, 0, 0)),
+                pl.BlockSpec((group, BLOCK, columns), lambda b, ids: (b, 0, 0)),
                 pl.BlockSpec((workers, slots, BLOCK, columns), lambda b, ids: (0, 0, 0, 0)),
             ],
             out_specs=(
-                pl.BlockSpec((1, BLOCK, columns), lambda b, ids: (b, 0, 0)),
-                pl.BlockSpec((1, 1, LANES), lambda b, ids: (b, 0, 0)),
+                pl.BlockSpec((group, BLOCK, columns), lambda b, ids: (b, 0, 0)),
+                pl.BlockSpec((group, 1, LANES), lambda b, ids: (b, 0, 0)),
             ),
         ),
         compiler_params=params(dimension_semantics=("arbitrary",)),
@@ -289,6 +291,7 @@
     ids = jnp.sum(jnp.where(chosen, jnp.arange(blocks, dtype=jnp.int32)[None, :], 0), axis=1)
     filled = jnp.sum(chosen.astype(jnp.int32), axis=1)
     rows = lax.all_gather(row, "dp")
+    rows, routes, gate_probs = lax.optimization_barrier((rows, routes, gate_probs))
     table = jnp.where(rows == 1, jnp.cumsum(rows, axis=1) - 1, -1)
 
     arrived = dispatch(routes.T, gate_probs.T, cotangents, experts, capacity).reshape(-1, width)

time: 325 us -> 282 us (0.87)
  waiting for transfers between devices: 0.01 us -> 147 us
  blocking collectives: 152 us -> 22.5 us
  Pallas kernels: 158 us -> 101 us
    all_to_all x1, waiting for transfers between devices: 0.01 us -> 147 us  [local(): lax.all_to_all(packed, 'dp', split_axis=0, concat_axis=0, tiled=True)]
    all_gather x1, blocking collectives: 152 us -> 22.5 us  [local(): rows = lax.all_gather(row, 'dp')]
    pallas_call x1, Pallas kernels: 48.5 us -> 9.52 us  [shared_total(): pl.pallas_call(functools.partial(total_kernel, n), out_shape=jax.ShapeDty...]
    pallas_call x1, Pallas kernels: 34.7 us -> 16.6 us  [add_landed(): pl.pallas_call(functools.partial(add_kernel, workers, group), out_shape=(...]
  transfers between devices with their start and end apart: 1 -> 1, of which waited for: 0 -> 1; matrix products, arithmetic and copies ran while one was open for 0% -> 0% of each run, Pallas kernels for 11% -> 13%
where the time goes in v2:
time: 282 us; the launch traced here: 281 us
  waiting for transfers between devices  147 us (52%)
  Pallas kernels  101 us (36%)
  blocking collectives  22.5 us (8%)
  starting transfers between devices  4.96 us (2%)
  other arithmetic  3.81 us (1%)
    all_to_all x1, waiting for transfers between devices, local(): lax.all_to_all(packed, 'dp', split_axis=0, concat_axis=0, tiled=True)  147 us
    pallas_call x1, Pallas kernels, block_norms(): pl.pallas_call(functools.partial(norms_kernel, group), out_shape=jax.Shap...  36.3 us
    all_gather x1, blocking collectives, local(): rows = lax.all_gather(row, 'dp')  22.5 us
    pallas_call x1, Pallas kernels, dispatch(): pl.pallas_call(functools.partial(exchange_kernel, n), out_shape=shape, in...  18.5 us
    pallas_call x1, Pallas kernels, picked_blocks(): pl.pallas_call(functools.partial(picked_kernel, parts), out_shape=jax.Sha...  17.1 us
    pallas_call x1, Pallas kernels, add_landed(): pl.pallas_call(functools.partial(add_kernel, workers, group), out_shape=(...  16.6 us
    pallas_call x1, Pallas kernels, shared_total(): pl.pallas_call(functools.partial(total_kernel, n), out_shape=jax.ShapeDty...  9.52 us
  transfers between devices with their start and end apart: 1, of which 1 were waited for; matrix products, arithmetic and copies ran while one was open for 0% of the time, Pallas kernels for 13%

profile of v2, /device:TPU:0, one launch (start us, length us, event | category | flops | bytes accessed | tf_op | source)
XLA Modules:
  0.0 280.9 jit_solution(6837814111377925034)
XLA Ops:
  0.6 0.7 compare_bitcast_fusion
  1.3 22.5 %all-gather = s32[8,1,56]{2,1,0:T(1,128)S(1)} all-gather(s32[1,1,56]{2,1,0:T(1,128)} %param.14), channel_id=2, replica_groups=mesh['expert'=4,'dp'=8] {'dp'}, dimensions={0}, use_global_device_ids=true | all-gather | bytes 2016 | tf_op jit(solution)/shard_map/all_gather | solution.py:293
  23.8 0.7 copy.15
  24.5 0.1 reduce-window.8
  24.6 0.1 reduce
  24.7 2.8 table.1.table_ref
  27.5 18.5 %exchange.1 = bf16[4,80,2048]{2,1,0:T(8,128)(2,1)} custom-call(bf16[4,80,2048]{2,1,0:T(8,128)(2,1)} %table.1.table_ref), custom_call_target="tpu_custom_call" | custom-call | tf_op jit(solution)/shard_map/exchange/pallas_call | solution.py:90
  46.0 0.2 select_reduce_fusion
  46.2 0.6 pad_add_fusion.picked_ref
  46.7 17.1 %picked.1 = bf16[8,16,128,256]{3,2,1,0:T(8,128)(2,1)} custom-call(s32[2,16]{1,0:T(2,128)} %pad_add_fusion.picked_ref, bf16[320,7168]{1,0:T(8,128)(2,1)} %bitcast.21, bf16[320,7168]{1,0:T(8,128)(2,1)} %bitcast.23, bf16[320,2048]{1,0:T(8,128)(2,1)} %bitcast.19, bf16[320,2048]{1,0:T(8,128)(2,1)} %bitcast.25), custom_call_target="tpu_custom_call" | custom-call | flops 5368709120 | bytes 16777216 | tf_op jit(solution)/shard_map/picked/pallas_call | solution.py:125
  63.9 5.0 %all-to-all-start = ((bf16[8,16,128,256]{3,2,1,0:T(8,128)(2,1)}), bf16[8,16,128,256]{3,2,1,0:T(8,128)(2,1)}, u32[]{:S(2)}, u32[]{:S(2)}) async-start(bf16[8,16,128,256]{3,2,1,0:T(8,128)(2,1)} %picked.1), calls=%async_computation | async-start | bytes 16777216 | tf_op jit(solution)/shard_map/all_to_all | solution.py:299
  68.8 0.2 reduce_window_sum.18
  69.0 0.6 add_select_fusion.table_ref
  69.6 36.3 %norms.1 = f32[56,1,128]{2,1,0:T(1,128)} custom-call(bf16[320,7168]{1,0:T(8,128)(2,1)} %bitcast.22, bf16[320,7168]{1,0:T(8,128)(2,1)} %bitcast.24, bf16[320,2048]{1,0:T(8,128)(2,1)} %bitcast.20, bf16[320,2048]{1,0:T(8,128)(2,1)} %bitcast.26), custom_call_target="tpu_custom_call" | custom-call | flops 18790481920 | bytes 9175040 | tf_op jit(solution)/shard_map/norms/pallas_call | solution.py:171
  106.0 147.5 %all-to-all-done.landed_ref = bf16[8,16,128,256]{3,2,1,0:T(8,128)(2,1)} async-done(((bf16[8,16,128,256]{3,2,1,0:T(8,128)(2,1)}), bf16[8,16,128,256]{3,2,1,0:T(8,128)(2,1)}, u32[]{:S(2)}, u32[]{:S(2)}) %all-to-all-start) | async-done | bytes 8388640 | tf_op jit(solution)/shard_map/all_to_all | solution.py:299
  253.4 0.0 copy-start
  253.4 16.6 %addlanded.1 = (f32[56,128,256]{2,1,0:T(8,128)}, f32[56,1,128]{2,1,0:T(1,128)}) custom-call(s32[8,56]{1,0:T(8,128)} %add_select_fusion.table_ref, f32[56,128,256]{2,1,0:T(8,128)} %bitcast.18, bf16[8,16,128,256]{3,2,1,0:T(8,128)(2,1)} %all-to-all-done.landed_ref), custom_call_target="tpu_custom_call" | custom-call | flops 7340032 | bytes 18350080 | tf_op jit(solution)/shard_map/addlanded/pallas_call | solution.py:213
  270.0 9.5 %total.1 = f32[56,128]{1,0:T(8,128)} custom-call(f32[56,128]{1,0:T(8,128)} %bitcast.30), custom_call_target="tpu_custom_call" | custom-call | tf_op jit(solution)/shard_map/total/pallas_call | solution.py:261
  279.5 0.0 copy-done
  279.5 0.9 subtract_reduce_fusion
  280.4 0.5 multiply_bitcast_fusion
  (1 shorter events, 0.0 us)
Async XLA Ops:
  63.9 189.5 %all-to-all-start = ((bf16[8,16,128,256]{3,2,1,0:T(8,128)(2,1)}), bf16[8,16,128,256]{3,2,1,0:T(8,128)(2,1)}, u32[]{:S(2)}, u32[]{:S(2)}) async-start(bf16[8,16,128,256]{3,2,1,0:T(8,128)(2,1)} %picked.1), calls=%async_computation | async-start | bytes 16777216 | tf_op jit(solution)/shard_map/all_to_all | solution.py:299
  253.4 26.1 %copy-start = (f32[56,1,128]{2,1,0:T(1,128)S(1)}, f32[56,1,128]{2,1,0:T(1,128)}, u32[]{:S(2)}) copy-start(f32[56,1,128]{2,1,0:T(1,128)} %norms.1) | copy-start | bytes 86020
